TPU v7x, 128 devices: a whole 4x4x4 slice. The times are simulated.
128 devices in a mesh: gx: 4 (over x_hi, core), gy: 32 (over x_lo, z, y).
Axes of the slice: x: 4 (x_hi: 2, x_lo: 2; x = x_hi * 2 + x_lo), y: 4, z: 4, core: 2. Of those that a mesh axis runs over, the one named last changes fastest.
Arguments:
- activations: bfloat16 [4096, 8192], P('gx', 'gy'), may hold values from -12 to 12
- out_grads: bfloat16 [4096, 16384], P('gx', 'gy'), may hold values from -12 to 12
- left_roots: float32 [128, 1024, 1024], P(('gx', 'gy')), may hold values from -20 to 20, as said below
- right_roots: float32 [128, 1024, 1024], P(('gx', 'gy')), may hold values from -20 to 20, as said below
Outputs:
- update: bfloat16 [8192, 16384], P(None, 'gy')
Inputs may be any that keep to these rules, and one draw needn't show every extreme that they name: `left_roots`: each block is symmetric positive definite. `right_roots`: each block is symmetric positive definite.
All inputs are finite; a program needn't handle non-finite values.
Results may differ from a plain program's by a relative error of at most 0.001.
Values may be sent and summed in bfloat16 or wider, within the bound.
A program may use at most 128 MiB of HBM per device.

v0:
```python
import jax
import jax.numpy as jnp
from jax import lax
from jax.sharding import PartitionSpec as P

epsilon = 1e-06


def partner_2(block, axis, distance):
    count = lax.axis_size(axis)
    route = []
    for low in range(count):
        high = low | 1 << distance
        if high != low and high < count:
            route += [(low, high), (high, low)]
    return lax.ppermute(block, axis, route)


def local(activations, out_grads, left_roots, right_roots):
    block_size = left_roots.shape[1]
    half_width = block_size // 2
    parity = lax.axis_index("gy") % 2
    is_even = parity == 0
    gathered = lax.all_gather(activations, "gy", axis=1, tiled=True)
    tok_count = gathered.shape[0]
    partner = partner_2(out_grads, "gy", 0)
    columns = jnp.concatenate(
        [jnp.where(is_even, out_grads, partner), jnp.where(is_even, partner, out_grads)], axis=1
    )
    groups = gathered.reshape(tok_count, -1, 2, block_size)
    chosen = lax.dynamic_index_in_dim(groups, parity, 2, keepdims=False).reshape(tok_count, -1)
    grad_block = lax.psum_scatter(
        lax.dot_general(
            chosen, columns, (((0,), (0,)), ((), ())), preferred_element_type=jnp.float32
        ),
        "gx",
        scatter_dimension=0,
        tiled=True,
    )
    shaped = jnp.dot(
        jnp.dot(left_roots[0], grad_block, precision=lax.Precision.HIGHEST),
        right_roots[0],
        precision=lax.Precision.HIGHEST,
    )
    graft = jnp.sqrt(jnp.mean(grad_block * grad_block) + epsilon) / jnp.sqrt(
        jnp.mean(shaped * shaped) + epsilon
    )
    finished = (shaped * graft).astype(jnp.bfloat16)
    own_part = lax.dynamic_slice_in_dim(finished, parity * half_width, half_width, 1)
    far_part = lax.dynamic_slice_in_dim(finished, (1 - parity) * half_width, half_width, 1)
    received = partner_2(far_part, "gy", 0)
    upper_rows = jnp.where(is_even, own_part, received)
    lower_rows = jnp.where(is_even, received, own_part)
    paired = jnp.concatenate([upper_rows, lower_rows], axis=0)
    return lax.all_gather(paired, "gx", axis=0, tiled=True)


def solution(mesh):
    in_specs = (
        P("gx", "gy"),
        P("gx", "gy"),
        P(("gx", "gy"), None, None),
        P(("gx", "gy"), None, None),
    )
    out_specs = P(None, "gy")
    return jax.shard_map(local, mesh=mesh, in_specs=in_specs, out_specs=out_specs, check_vma=False)
```

profile of v0, /device:TPU:1, one launch (start us, length us, event | category | flops | bytes accessed | tf_op | source)
XLA Modules:
  0.0 525.2 jit_solution(1484673411043954595)
XLA Ops:
  6.5 0.0 all-gather.3.cloned.1.call-start
  6.5 2.0 copy.5
  8.6 0.0 all-gather.3.cloned.1.call-update
  8.6 0.0 reduce-scatter.2.cloned.1.call-start
  8.7 2.2 collective-permute-start
  10.8 34.2 %collective-permute-done = bf16[1024,512]{1,0:T(8,128)(2,1)S(1)} collective-permute-done((bf16[1024,512]{1,0:T(8,128)(2,1)}, bf16[1024,512]{1,0:T(8,128)(2,1)S(1)}, u32[]{:S(2)}, u32[]{:S(2)}) %collective-permute-start) | collective-permute-done | bytes 1048608 | tf_op jit(solution)/shard_map/ppermute | solution.py:16
  45.0 1.4 broadcast_select_fusion.3
  46.4 167.7 %all-gather.3.cloned.1.call-done = bf16[1024,8192]{0,1:T(8,128)(2,1)} async-done(((bf16[1024,256]{0,1:T(8,128)(2,1)}), bf16[1024,8192]{0,1:T(8,128)(2,1)}) %all-gather.3.cloned.1.call-update) | async-done | bytes 16777232 | tf_op jit(solution)/shard_map/all_gather | solution.py:24
  214.0 7.8 %constant_dynamic-slice_fusion.1 = bf16[1024,4,1,1024]{0,3,2,1:T(8,128)(2,1)} fusion(bf16[1024,4,2,1024]{0,3,2,1:T(8,128)(2,1)} %bitcast.14, s32[]{:T(128)S(6)} %select_n.39), kind=kLoop, calls=%fused_computation.17 | loop fusion | bytes 16777220 | tf_op jit(solution)/shard_map/jit(dynamic_index_in_dim)/dynamic_slice | solution.py:31
  221.8 14.5 %fusion.4 = f32[4096,1024]{1,0:T(8,128)} fusion(bf16[1024,4096]{0,1:T(8,128)(2,1)} %bitcast.13, bf16[1024,512]{1,0:T(8,128)(2,1)S(1)} %get-tuple-element.8, bf16[1024,512]{1,0:T(8,128)(2,1)S(1)} %get-tuple-element.7), kind=kOutput, calls=%fused_computation.7 | convolution fusion | flops 8594128896 | bytes 27262976 | tf_op jit(solution)/shard_map/dot_general | solution.py:33
  236.3 0.0 reduce-scatter.2.cloned.1.call-update
  236.3 0.0 all-gather.5.cloned.1.call-start
  236.4 130.5 %reduce-scatter.2.cloned.1.call-done = f32[1024,1024]{1,0:T(8,128)} async-done(((f32[4096,1024]{1,0:T(8,128)}), f32[1024,1024]{1,0:T(8,128)}) %reduce-scatter.2.cloned.1.call-update) | async-done | bytes 4194320 | tf_op jit(solution)/shard_map/reduce_scatter | solution.py:32
  366.9 0.0 copy-start
  366.9 30.1 %fusion.2 = f32[1024,1024]{1,0:T(8,128)S(1)} fusion(f32[1024,1024]{1,0:T(8,128)} %reduce-scatter.2.cloned.1.call-done, f32[1,1024,1024]{2,1,0:T(8,128)} %param.6), kind=kOutput, calls=%fused_computation.2 | convolution fusion | flops 12884901888 | bytes 12582912 | tf_op jit(solution)/shard_map/dot_general | solution.py:41
  397.0 0.0 copy-done
  397.0 15.7 %multiply_reduce_fusion = (f32[]{:T(128)}, f32[1024,1024]{1,0:T(8,128)}) fusion(f32[1024,1024]{1,0:T(8,128)S(1)} %fusion.2, f32[1,1024,1024]{2,1,0:T(8,128)S(1)} %copy-done), kind=kOutput, calls=%fused_computation.5 | convolution fusion | flops 12886999040 | bytes 12582916 | tf_op jit(solution)/shard_map/dot_general | solution.py:40
  413.5 4.0 multiply_reduce_fusion.1
  418.2 2.8 multiply_convert_fusion
  420.9 1.1 constant_dynamic-slice_fusion
  422.0 1.2 collective-permute-start.1
  423.2 22.8 %collective-permute-done.1 = bf16[1024,512]{1,0:T(8,128)(2,1)S(1)} collective-permute-done((bf16[1024,512]{1,0:T(8,128)(2,1)}, bf16[1024,512]{1,0:T(8,128)(2,1)S(1)}, u32[]{:S(2)}, u32[]{:S(2)}) %collective-permute-start.1) | collective-permute-done | bytes 1048608 | tf_op jit(solution)/shard_map/ppermute | solution.py:16
  446.1 0.5 broadcast_select_fusion.1
  446.6 1.5 pad_maximum_fusion
  448.0 0.0 all-gather.5.cloned.1.call-update
  448.0 63.3 %all-gather.5.cloned.1.call-done = bf16[8192,512]{1,0:T(8,128)(2,1)} async-done(((bf16[2048,512]{1,0:T(8,128)(2,1)}), bf16[8192,512]{1,0:T(8,128)(2,1)}) %all-gather.5.cloned.1.call-update) | async-done | bytes 8388624 | tf_op jit(solution)/shard_map/all_gather | solution.py:55
  511.4 7.3 %copy.7 = bf16[8192,512]{1,0:T(8,128)(2,1)} copy(bf16[8192,512]{1,0:T(8,128)(2,1)} %all-gather.5.cloned.1.call-done) | data formatting | bytes 16777216
Async XLA Ops:
  6.5 207.5 %all-gather.3.cloned.1.call-start = ((), (), s32[]{:S(2)}) async-start(), calls=%async_computation.1 | async-start | bytes 17301504 | tf_op jit(solution)/shard_map/all_gather | solution.py:24
  8.6 358.3 %reduce-scatter.2.cloned.1.call-start = ((), (), s32[]{:S(2)}) async-start(), calls=%async_computation.2 | async-start | bytes 20971520 | tf_op jit(solution)/shard_map/reduce_scatter | solution.py:32
  8.7 36.4 %collective-permute-start = (bf16[1024,512]{1,0:T(8,128)(2,1)}, bf16[1024,512]{1,0:T(8,128)(2,1)S(1)}, u32[]{:S(2)}, u32[]{:S(2)}) collective-permute-start(bf16[1024,512]{1,0:T(8,128)(2,1)} %param.5), channel_id=1, source_target_pairs={{0,1},{1,0},{2,3},{3,2},{4,5},{5,4},{6,7},{7,6},{8,9},{9,8},{10,11... | collective-permute-start | bytes 3145736 | tf_op jit(solution)/shard_map/ppermute | solution.py:16
  236.3 275.1 %all-gather.5.cloned.1.call-start = ((), (), s32[]{:S(2)}) async-start(), calls=%async_computation.3 | async-start | bytes 10485760 | tf_op jit(solution)/shard_map/all_gather | solution.py:55
  366.9 30.1 %copy-start = (f32[1,1024,1024]{2,1,0:T(8,128)S(1)}, f32[1,1024,1024]{2,1,0:T(8,128)}, u32[]{:S(2)}) copy-start(f32[1,1024,1024]{2,1,0:T(8,128)} %param.7) | copy-start | bytes 12582916
  422.0 24.1 %collective-permute-start.1 = (bf16[1024,512]{1,0:T(8,128)(2,1)}, bf16[1024,512]{1,0:T(8,128)(2,1)S(1)}, u32[]{:S(2)}, u32[]{:S(2)}) collective-permute-start(bf16[1024,512]{1,0:T(8,128)(2,1)} %constant_dynamic-slice_fusion), channel_id=1, source_target_pairs={{0,1},{1,0},{2,3},{3,2},{4,5},{5,4},{6,7},{7,6},{8,9},{9,8},{10,11... | collective-permute-start | bytes 3145736 | tf_op jit(solution)/shard_map/ppermute | solution.py:16
Sparse Core Ops, SparseCore 0:
  9.0 205.0 all-gather.2
  236.4 130.4 reduce-scatter.1
  448.2 63.1 all-gather.4
where the time goes:
time: 526 us; the launch traced here: 525 us
  waiting for transfers between devices  419 us (80%)
  matrix products  60.3 us (11%)
  local copies, waits for them, and re-layouts  18.2 us (3%)
  between operations  14.6 us (3%)
  other arithmetic  10 us (2%)
    all_gather x1, waiting for transfers between devices, local(): gathered = lax.all_gather(activations, 'gy', axis=1, tiled=True)  168 us
    reduce_scatter x1, waiting for transfers between devices, local(): lax.psum_scatter(lax.dot_general(chosen, columns, (((0,), (0,)), ((), ())...  131 us
    all_gather x1, waiting for transfers between devices, local(): return lax.all_gather(paired, 'gx', axis=0, tiled=True)  63.3 us
    ppermute x2, waiting for transfers between devices, partner_2(): return lax.ppermute(block, axis, route)  57 us
    dot_general x1, matrix products, local(): jnp.dot(left_roots[0], grad_block, precision=lax.Precision.HIGHEST)  30.1 us
    dot_general x1, matrix products, local(): jnp.dot(jnp.dot(left_roots[0], grad_block, precision=lax.Precision.HIGHES...  15.7 us
    dot_general x1, matrix products, local(): lax.dot_general(chosen, columns, (((0,), (0,)), ((), ())), preferred_elem...  14.5 us
  transfers between devices with their start and end apart: 5, of which 5 were waited for; matrix products, arithmetic and copies ran while one was open for 0% of the time, Pallas kernels for 0%

commit v1 on v0

v1 whole, which is shorter than its diff:
```python
import functools

import jax
import jax.numpy as jnp
from jax import lax
from jax.experimental import pallas as pl
from jax.experimental.pallas import tpu as pltpu
from jax.sharding import PartitionSpec as P

epsilon = 1e-06
BF16 = jnp.bfloat16
F32 = jnp.float32
TOK = 1024
FEAT = 256
HALF = 512
BLK = 1024
GC = 2
OC = 4


def device(x, y, z, c):
    x, y, z = x % 4, y % 4, z % 4
    return ((x // 2) * 2 + c, (x % 2) * 16 + z * 4 + y)


def push(src, dst, send_sem, recv_sem, target):
    return pltpu.make_async_remote_copy(
        src_ref=src, dst_ref=dst, send_sem=send_sem, recv_sem=recv_sem,
        device_id=target, device_id_type=pl.DeviceIdType.MESH,
    )


def split(value):
    high = value.astype(BF16)
    return high, (value - high.astype(F32)).astype(BF16)


def mm(a, b):
    return jnp.dot(a, b, preferred_element_type=F32)


def kernel(
    act, cot, left, right, out,
    abuf, gbuf, l1, l2, r1, r2, sbuf, wbuf, gacc, g1, g2, gsq, ssq, fin,
    a_recv, x_send, y_send, up_send, down_send,
    g_recv, g_send, gf_send, gd_send, o_recv, o_send, od_send, l_sem, lg_sem, lo_sem,
):
    gx, gy = lax.axis_index("gx"), lax.axis_index("gy")
    x_hi, c = gx // 2, gx % 2
    x_lo, z, y = gy // 16, (gy // 4) % 4, gy % 4
    x = 2 * x_hi + x_lo
    p = y % 2
    y_pair = y + 1 - 2 * p
    odd = (y + z) % 2
    k_home = z // 2
    rel = (2 * c + p - z) % 4
    home = rel == 0
    other_core = device(x, y, z, 1 - c)
    across = device(x + 2, y, z, c)
    pair = device(x, y_pair, z, c)
    pair_across = device(x + 2, y_pair, z, c)

    load_left = pltpu.make_async_copy(left.at[0], sbuf, l_sem.at[0])
    load_right = pltpu.make_async_copy(right.at[0], wbuf, l_sem.at[1])
    load_left.start()
    load_right.start()

    barrier = pltpu.get_barrier_semaphore()
    greeted = [device(x + d, y, z, c) for d in (1, 2, 3)]
    greeted += [device(x, y + d, z, c) for d in (1, 2, 3)]
    greeted += [device(x, y + d, z, 1 - c) for d in (0, 1, 2, 3)]
    greeted += [device(x, y, z + 1, c), device(x, y, z + 3, c), pair_across]
    for target in greeted:
        pl.semaphore_signal(barrier, inc=1, device_id=target, device_id_type=pl.DeviceIdType.MESH)
    pl.semaphore_wait(barrier, len(greeted))

    def arrived(ref, sem):
        push(ref, ref, x_send.at[0], sem, other_core).wait_recv()

    keeps_home = jnp.logical_and(odd == 0, c == k_home)

    def x_slot(source):
        return jnp.where(keeps_home, 4 * y + 2 * source + c, 16 + source)

    own_slot = x_slot(x_hi)
    x_target = [2 * x_lo, 2 * x_lo + 1]
    for t in range(2):
        copy = push(act, abuf.at[own_slot], x_send.at[t], a_recv.at[own_slot], device(x_target[t], y, z, c))
        pl.when(x_target[t] != x)(copy.start)
    stays = pltpu.make_async_copy(act, abuf.at[own_slot], a_recv.at[own_slot])
    pl.when(x_lo == x_hi)(stays.start)

    g_own, g_far = 2 * x_hi + c, 2 * (1 - x_hi) + c
    rows = TOK // GC

    def g_part(g, h, j):
        return gbuf.at[g, h, pl.ds(rows * j, rows), :]

    def g_sem(g, h, j):
        return g_recv.at[(2 * g + h) * GC + j]

    keep_g = pltpu.make_async_copy(cot, gbuf.at[g_own, p], lg_sem)
    keep_g.start()
    g_sends = []
    for j in range(GC):
        for n, target in enumerate((pair, across, other_core)):
            copy = push(cot.at[pl.ds(rows * j, rows), :], g_part(g_own, p, j), g_send.at[n, j], g_sem(g_own, p, j), target)
            copy.start()
            g_sends.append(copy)

    y_copies = []
    for s in range(2):
        source = (x_hi + s) % 2
        slot = x_slot(source)
        arrived(abuf.at[slot], a_recv.at[slot])
        final = 4 * y + 2 * source + c
        for n, (when, dy) in enumerate(((odd == 1, 1), (odd == 1, 3), (odd == 0, 2))):
            copy = push(
                abuf.at[slot], abuf.at[final], y_send.at[n, s], a_recv.at[final], device(x, y + dy, z, k_home)
            )
            pl.when(when)(copy.start)
            y_copies.append((when, copy))
        copy = push(abuf.at[slot], abuf.at[final], y_send.at[3, s], a_recv.at[final], other_core)
        when = jnp.logical_and(odd == 0, c != k_home)
        pl.when(when)(copy.start)
        y_copies.append((when, copy))

    def split_roots(i, carry):
        part = pl.ds(pl.multiple_of(128 * i, 128), 128)
        l1[part, :], l2[part, :] = split(sbuf[part, :])
        r1[part, :], r2[part, :] = split(wbuf[part, :])
        return carry

    load_left.wait()
    load_right.wait()
    lax.fori_loop(0, 8, split_roots, 0)
    sbuf[...] = jnp.zeros_like(sbuf)
    gsq[...] = jnp.zeros_like(gsq)
    ssq[...] = jnp.zeros_like(ssq)

    above, below = device(x, y, z + 1, c), device(x, y, z + 3, c)

    def order(i):
        q = i // 4
        ys = (y + q + (q // 2) * (1 - 2 * (q % 2))) % 4
        g = 2 * ((x_hi + (i % 4) // 2) % 2) + i % 2
        return ys, g, 4 * ys + g

    def z_copies(i):
        _, _, slot = order(i)
        ref = abuf.at[slot]
        up = push(ref, ref, up_send.at[slot], a_recv.at[slot], above)
        down = push(ref, ref, down_send.at[slot], a_recv.at[slot], below)
        go_up = jnp.logical_or(home, jnp.logical_and(rel == 3, i % 2 == 0))
        go_down = jnp.logical_or(home, jnp.logical_and(rel == 1, i % 2 == 1))
        return (go_up, up), (go_down, down)

    def relay(i, carry=0):
        _, g, slot = order(i)
        held = jnp.logical_and(keeps_home, jnp.logical_and(i // 4 == 0, i % 2 == c))

        @pl.when(jnp.logical_not(held))
        def _():
            arrived(abuf.at[slot], a_recv.at[slot])

        for when, copy in z_copies(i):
            pl.when(when)(copy.start)
        return carry

    gf_sends, gd_sends = [], []

    def to_core(g, h, j):
        copy = push(g_part(g, h, j), g_part(g, h, j), gd_send.at[len(gd_sends)], g_sem(g, h, j), other_core)
        copy.start()
        gd_sends.append(copy)

    def cot_pair(j):
        arrived(g_part(g_own, 1 - p, j), g_sem(g_own, 1 - p, j))
        copy = push(g_part(g_own, 1 - p, j), g_part(g_own, 1 - p, j), gf_send.at[j], g_sem(g_own, 1 - p, j), across)
        copy.start()
        gf_sends.append(copy)
        to_core(g_own, 1 - p, j)

    def cot_far(h, j):
        arrived(g_part(g_far, h, j), g_sem(g_far, h, j))
        to_core(g_far, h, j)

    steps = [
        [0], [lambda: cot_pair(0)], [1, 2], [lambda: cot_pair(1), lambda: cot_far(p, 0)], [3, 4],
        [lambda: cot_far(p, 1)], [5, 6], [lambda: cot_far(1 - p, 0)], [7, 8], [lambda: cot_far(1 - p, 1)], [9],
    ]
    for group in steps:
        for step in group:
            if callable(step):
                step()
            else:
                relay(step)
    for g in range(2):
        for h in range(2):
            for j in range(GC):
                number = 2 * g + 1 - c
                arrived(g_part(number, h, j), g_sem(number, h, j))
    keep_g.wait()

    def piece(i, carry):
        ys, g, slot = order(i)

        @pl.when(i % 4 == 0)
        def _():
            gacc[...] = jnp.zeros_like(gacc)

        for h in range(2):
            gacc[:, pl.ds(HALF * h, HALF)] += lax.dot_general(
                abuf[slot], gbuf[g, h], (((0,), (0,)), ((), ())), preferred_element_type=F32
            )

        @pl.when(i % 4 == 3)
        def _():
            value = gacc[...]
            gsq[...] += jnp.sum(value * value, axis=0, keepdims=True)
            g1[...], g2[...] = split(value)
            columns = pl.ds(pl.multiple_of(FEAT * ys, FEAT), FEAT)

            def left_rows(r, inner):
                part = pl.ds(pl.multiple_of(256 * r, 256), 256)
                high = l1[part, columns]
                sbuf[part, :] += mm(high, g1[...]) + mm(high, g2[...]) + mm(l2[part, columns], g1[...])
                return inner

            lax.fori_loop(0, 4, left_rows, 0)

        return carry

    def relay_and_multiply(i, carry):
        relay(i)
        lax.fori_loop((i - 10) * 16 // 6, (i - 9) * 16 // 6, piece, 0)
        return carry

    lax.fori_loop(10, 16, relay_and_multiply, 0)

    def right_rows(r, carry):
        part = pl.ds(pl.multiple_of(256 * r, 256), 256)
        high, low = split(sbuf[part, :])
        for h in range(2):
            cols = pl.ds(HALF * h, HALF)
            value = mm(high, r1[:, cols]) + mm(high, r2[:, cols]) + mm(low, r1[:, cols])
            wbuf[part, cols] = value
            ssq[:, cols] += jnp.sum(value * value, axis=0, keepdims=True)
        return carry

    lax.fori_loop(0, 4, right_rows, 0)
    count = BLK * BLK
    graft = jnp.sqrt(jnp.sum(gsq[...], axis=1, keepdims=True) / count + epsilon) / jnp.sqrt(
        jnp.sum(ssq[...], axis=1, keepdims=True) / count + epsilon
    )

    block = 4 * x_hi + 2 * c + p
    orows = BLK // OC

    def o_part(number, j):
        return out.at[pl.ds(pl.multiple_of(BLK * number + orows * j, orows), orows), :]

    def o_sem(number, j):
        return o_recv.at[number * OC + j]

    o_sends = []
    for j in range(OC + 1):
        if j < OC:
            for h in range(2):
                fin[h, pl.ds(orows * j, orows), :] = (
                    wbuf[pl.ds(orows * j, orows), pl.ds(HALF * h, HALF)] * graft
                ).astype(BF16)
        if j > 0:
            i = j - 1
            mine = fin.at[p, pl.ds(orows * i, orows), :]
            theirs = fin.at[1 - p, pl.ds(orows * i, orows), :]
            for n, (src, target) in enumerate(
                ((mine, across), (theirs, pair_across), (theirs, pair), (mine, other_core))
            ):
                copy = push(src, o_part(block, i), o_send.at[n, i], o_sem(block, i), target)
                copy.start()
                o_sends.append(copy)
            copy = pltpu.make_async_copy(mine, o_part(block, i), lo_sem.at[i])
            copy.start()
    od_sends = []
    p_core = 2 * c
    far = 4 * (1 - x_hi)
    for j in range(OC):
        for n, number in enumerate((4 * x_hi + p_core + 1 - p, far + p_core + p, far + p_core + 1 - p)):
            arrived(o_part(number, j), o_sem(number, j))
            copy = push(o_part(number, j), o_part(number, j), od_send.at[n, j], o_sem(number, j), other_core)
            copy.start()
            od_sends.append(copy)

    for j in range(OC):
        for number in (0, 1, 4, 5):
            arrived(o_part(number + 2 * (1 - c), j), o_sem(number + 2 * (1 - c), j))
        pltpu.make_async_copy(fin.at[p, pl.ds(orows * j, orows), :], o_part(block, j), lo_sem.at[j]).wait()
    for t in range(2):
        copy = push(act, abuf.at[own_slot], x_send.at[t], a_recv.at[own_slot], device(x_target[t], y, z, c))
        pl.when(x_target[t] != x)(copy.wait_send)
    for when, copy in y_copies:
        pl.when(when)(copy.wait_send)

    def drain(i, carry):
        for when, copy in z_copies(i):
            pl.when(when)(copy.wait_send)
        return carry

    lax.fori_loop(0, 16, drain, 0)
    for copy in g_sends + gf_sends + gd_sends + o_sends + od_sends:
        copy.wait_send()


def local(act, cot, left, right):
    dma = pltpu.SemaphoreType.DMA
    anywhere = pl.BlockSpec(memory_space=pl.ANY)
    return pl.pallas_call(
        kernel,
        out_shape=jax.ShapeDtypeStruct((8 * BLK, HALF), BF16),
        in_specs=[anywhere] * 4,
        out_specs=anywhere,
        scratch_shapes=[
            pltpu.VMEM((18, TOK, FEAT), BF16),
            pltpu.VMEM((4, 2, TOK, HALF), BF16),
            pltpu.VMEM((BLK, BLK), BF16), pltpu.VMEM((BLK, BLK), BF16),
            pltpu.VMEM((BLK, BLK), BF16), pltpu.VMEM((BLK, BLK), BF16),
            pltpu.VMEM((BLK, BLK), F32), pltpu.VMEM((BLK, BLK), F32),
            pltpu.VMEM((FEAT, BLK), F32),
            pltpu.VMEM((FEAT, BLK), BF16), pltpu.VMEM((FEAT, BLK), BF16),
            pltpu.VMEM((1, BLK), F32), pltpu.VMEM((1, BLK), F32),
            pltpu.VMEM((2, BLK, HALF), BF16),
            dma((18,)), dma((2,)), dma((4, 2)), dma((16,)), dma((16,)),
            dma((8 * GC,)), dma((3, GC)), dma((GC,)), dma((3 * GC,)),
            dma((8 * OC,)), dma((4, OC)), dma((3, OC)), dma((2,)), dma, dma((OC,)),
        ],
        compiler_params=pltpu.CompilerParams(
            collective_id=0, has_side_effects=True, vmem_limit_bytes=62 * 1024 * 1024
        ),
        name="shampoo",
    )(act, cot, left, right)


def solution(mesh):
    in_specs = (P("gx", "gy"), P("gx", "gy"), P(("gx", "gy"), None, None), P(("gx", "gy"), None, None))
    return jax.shard_map(local, mesh=mesh, in_specs=in_specs, out_specs=P(None, "gy"), check_vma=False)
```

time: 526 us -> 205 us (0.39)
  waiting for transfers between devices: 419 us -> 0 us
  Pallas kernels: 0 us -> 198 us
  matrix products: 60.3 us -> 0 us
  between operations: 14.6 us -> 0.01 us
  local copies, waits for them, and re-layouts: 18.2 us -> 7.32 us
  other arithmetic: 10 us -> 0 us
    all_gather x2 -> x0, waiting for transfers between devices: 231 us -> none  [the longest x1 168 us: local(): gathered = lax.all_gather(activations, 'gy', axis=1, tiled=True)]
    pallas_call x0 -> x1, Pallas kernels: none -> 198 us  [local(): pl.pallas_call(kernel, out_shape=jax.ShapeDtypeStruct((8 * BLK, HALF), BF...]
    reduce_scatter x1 -> x0, waiting for transfers between devices: 131 us -> none  [local(): lax.psum_scatter(lax.dot_general(chosen, columns, (((0,), (0,)), ((), ())...]
    dot_general x3 -> x0, matrix products: 60.3 us -> none  [the longest x1 30.1 us: local(): jnp.dot(left_roots[0], grad_block, precision=lax.Precision.HIGHEST)]
    ppermute x2 -> x0, waiting for transfers between devices: 57 us -> none  [partner_2(): return lax.ppermute(block, axis, route)]
    dynamic_slice x2 -> x0, local copies, waits for them, and re-layouts: 8.84 us -> none  [the longest x1 7.76 us: local(): lax.dynamic_index_in_dim(groups, parity, 2, keepdims=False)]
  transfers between devices with their start and end apart: 5 -> 0, of which waited for: 5 -> 0; matrix products, arithmetic and copies ran while one was open for 0% -> 0% of each run, Pallas kernels for 0% -> 0%
where the time goes in v1:
time: 205 us
  Pallas kernels  198 us (97%)
  local copies, waits for them, and re-layouts  7.32 us (4%)
    pallas_call x1, Pallas kernels, local(): pl.pallas_call(kernel, out_shape=jax.ShapeDtypeStruct((8 * BLK, HALF), BF...  198 us
    unnamed x1, local copies, waits for them, and re-layouts  7.32 us

profile of v1, /device:TPU:1, one launch (start us, length us, event | category | flops | bytes accessed | tf_op | source)
XLA Modules:
  0.0 205.1 jit_solution(12308762159111214744)
XLA Ops:
  0.0 197.8 %shampoo.1 = bf16[8192,512]{1,0:T(8,128)(2,1)} custom-call(bf16[1024,256]{1,0:T(8,128)(2,1)} %act.1, bf16[1024,512]{1,0:T(8,128)(2,1)} %cot.1, f32[1,1024,1024]{2,1,0:T(8,128)} %left.1, f32[1,1024,1024]{2,1,0:T(8,128)} %right.1), custom_call_target="tpu_custom_call" | custom-call | tf_op jit(solution)/shard_map/shampoo/pallas_call | solution.py:318
  197.8 7.3 %copy.6 = bf16[8192,512]{1,0:T(8,128)(2,1)} copy(bf16[8192,512]{1,0:T(8,128)(2,1)} %shampoo.1) | data formatting | bytes 16777216

commit v2 on v1

v2 whole, which is shorter than its diff:
```python
import functools

import jax
import jax.numpy as jnp
from jax import lax
from jax.experimental import pallas as pl
from jax.experimental.pallas import tpu as pltpu
from jax.sharding import PartitionSpec as P

epsilon = 1e-06
BF16 = jnp.bfloat16
F32 = jnp.float32
TOK = 1024
FEAT = 256
HALF = 512
BLK = 1024
CH = 256
LAST = 3
GC = 4
OC = 4


def device(x, y, z, c):
    x, y, z = x % 4, y % 4, z % 4
    return ((x // 2) * 2 + c, (x % 2) * 16 + z * 4 + y)


def push(src, dst, send_sem, recv_sem, target):
    return pltpu.make_async_remote_copy(
        src_ref=src, dst_ref=dst, send_sem=send_sem, recv_sem=recv_sem,
        device_id=target, device_id_type=pl.DeviceIdType.MESH,
    )


def split(value):
    high = value.astype(BF16)
    return high, (value - high.astype(F32)).astype(BF16)


def mm(a, b):
    return jnp.dot(a, b, preferred_element_type=F32)


def kernel(
    act, cot, left, right, out,
    abuf, gbuf, l1, l2, r1, r2, sbuf, wbuf, gacc, g1, g2, gsq, ssq, fin,
    x_recv, x_send, y_send, a_recv, up_send, down_send, z_recv, z_send, t_recv, t_send,
    g_recv, g_send, gf_send, gd_send, o_recv, o_send, od_send, l_sem, lg_sem, lo_sem,
):
    gx, gy = lax.axis_index("gx"), lax.axis_index("gy")
    x_hi, c = gx // 2, gx % 2
    x_lo, z, y = gy // 16, (gy // 4) % 4, gy % 4
    x = 2 * x_hi + x_lo
    p = y % 2
    y_pair = y + 1 - 2 * p
    odd = (y + z) % 2
    k_home = z // 2
    mine_z = 2 * c + p
    rel = (mine_z - z) % 4
    home = rel == 0
    other_core = device(x, y, z, 1 - c)
    across = device(x + 2, y, z, c)
    pair = device(x, y_pair, z, c)
    pair_across = device(x + 2, y_pair, z, c)
    above, below = device(x, y, z + 1, c), device(x, y, z + 3, c)

    load_left = pltpu.make_async_copy(left.at[0], sbuf, l_sem.at[0])
    load_right = pltpu.make_async_copy(right.at[0], wbuf, l_sem.at[1])

    barrier = pltpu.get_barrier_semaphore()
    greeted = [device(x + d, y, z, c) for d in (1, 2, 3)]
    greeted += [device(x, y + d, z, c) for d in (1, 2, 3)]
    greeted += [device(x, y + d, z, 1 - c) for d in (0, 1, 2, 3)]
    greeted += [above, below, pair_across]
    for target in greeted:
        pl.semaphore_signal(barrier, inc=1, device_id=target, device_id_type=pl.DeviceIdType.MESH)
    pl.semaphore_wait(barrier, len(greeted))

    def arrived(ref, sem):
        push(ref, ref, x_send.at[0, 0], sem, other_core).wait_recv()

    finals = []

    def start(copy, when=None):
        if when is None:
            copy.start()
        else:
            pl.when(when)(copy.start)
        finals.append((when, copy))

    def a_rows(slot, t):
        return abuf.at[pl.ds(pl.multiple_of(TOK * slot + CH * t, CH), CH), :]

    def x_slot(source):
        return jnp.where(home, 4 * y + 2 * source + c, 16 + source)

    own_slot = x_slot(x_hi)
    for t in (LAST, 0, 1, 2):
        src = act.at[pl.ds(CH * t, CH), :]
        for n in range(2):
            target = 2 * x_lo + n
            start(
                push(src, a_rows(own_slot, t), x_send.at[n, t], x_recv.at[x_hi, t], device(target, y, z, c)),
                target != x,
            )
        stays = pltpu.make_async_copy(src, a_rows(own_slot, t), x_recv.at[x_hi, t])
        pl.when(x_lo == x_hi)(stays.start)

    g_own, g_far = 2 * x_hi + c, 2 * (1 - x_hi) + c

    def g_part(g, h, j):
        return gbuf.at[g, h, pl.ds(CH * j, CH), :]

    def g_sem(g, h, j):
        return g_recv.at[(2 * g + h) * GC + j]

    def cot_own(n, target, j):
        start(push(cot.at[pl.ds(CH * j, CH), :], g_part(g_own, p, j), g_send.at[n, j], g_sem(g_own, p, j), target))

    for j in range(GC):
        cot_own(0, across, j)
    for j in range(GC):
        cot_own(1, other_core, j)
    keep_g = pltpu.make_async_copy(cot, gbuf.at[g_own, p], lg_sem)
    keep_g.start()
    load_left.start()
    load_right.start()

    def t_rows(zs, source):
        final = TOK * (4 * y + 2 * source + c) + CH * LAST
        waits = jnp.where(zs == z, TOK * (16 + source) + CH * LAST, TOK * 18 + CH * (2 * zs + source))
        return abuf.at[pl.ds(pl.multiple_of(jnp.where(zs == mine_z, final, waits), CH), CH), :]

    def t_land(zs, source):
        final = TOK * (4 * y + 2 * source + c) + CH * LAST
        waits = TOK * 18 + CH * (2 * zs + source)
        return abuf.at[pl.ds(pl.multiple_of(jnp.where(zs == mine_z, final, waits), CH), CH), :]

    sources = [(x_hi + s) % 2 for s in range(2)]
    for s, source in enumerate(sources):
        arrived(a_rows(x_slot(source), LAST), x_recv.at[source, LAST])
        ref = t_rows(z, source)
        start(push(ref, t_land(z, source), z_send.at[0, s], z_recv.at[2 * z + source], above))
        start(push(ref, t_land(z, source), z_send.at[1, s], z_recv.at[2 * z + source], below))

    def along_y(t):
        for s, source in enumerate(sources):
            slot = x_slot(source)
            arrived(a_rows(slot, t), x_recv.at[source, t])
            final = 4 * y + 2 * source + c
            for n, (when, dy) in enumerate(((odd == 1, 1), (odd == 1, 3), (odd == 0, 2))):
                start(
                    push(
                        a_rows(slot, t), a_rows(final, t), y_send.at[n, s, t], a_recv.at[final * 3 + t],
                        device(x, y + dy, z, k_home),
                    ),
                    when,
                )
            start(
                push(a_rows(slot, t), a_rows(final, t), y_send.at[3, s, t], a_recv.at[final * 3 + t], other_core),
                jnp.logical_and(odd == 0, c != k_home),
            )

    def source_y(q):
        return (y + q + (q // 2) * (1 - 2 * (q % 2))) % 4

    def order(i):
        t, q = i // 16, (i // 4) % 4
        g = 2 * ((x_hi + (i % 4) // 2) % 2) + i % 2
        return t, q, 4 * source_y(q) + g

    def z_copies(i):
        t, _, slot = order(i)
        ref, number = a_rows(slot, t), slot * 3 + t
        up = push(ref, ref, up_send.at[number], a_recv.at[number], above)
        down = push(ref, ref, down_send.at[number], a_recv.at[number], below)
        go_up = jnp.logical_or(home, jnp.logical_and(rel == 3, i % 2 == 0))
        go_down = jnp.logical_or(home, jnp.logical_and(rel == 1, i % 2 == 1))
        return (go_up, up), (go_down, down)

    def relay(i, carry=0):
        t, q, slot = order(i)
        held = jnp.logical_and(home, jnp.logical_and(q == 0, i % 2 == c))

        @pl.when(jnp.logical_not(held))
        def _():
            arrived(a_rows(slot, t), a_recv.at[slot * 3 + t])

        for when, copy in z_copies(i):
            pl.when(when)(copy.start)
        return carry

    def relay_step(s):
        lax.fori_loop(4 * s, 4 * s + 4, relay, 0)

    def last_along_z():
        for s, (zs, source, target) in enumerate((((z + 3) % 4, 0, above), ((z + 1) % 4, 1, below))):
            ref = t_rows(zs, source)
            arrived(ref, z_recv.at[2 * zs + source])
            start(push(ref, t_land(zs, source), z_send.at[2, s], z_recv.at[2 * zs + source], target))

    def last_along_y():
        for zs, source in (((z + 3) % 4, 1), ((z + 1) % 4, 0), ((z + 2) % 4, 0), ((z + 2) % 4, 1)):
            arrived(t_rows(zs, source), z_recv.at[2 * zs + source])
        for source in range(2):
            final = 4 * y + 2 * source + c
            land = a_rows(final, LAST)
            near, there = 2 * c + p, 2 * (1 - c) + p
            near_odd, there_odd = 2 * c + 1 - p, 2 * (1 - c) + 1 - p
            for n, (zs, target) in enumerate((
                (there, other_core),
                (near_odd, device(x, y + 1, z, c)), (near_odd, device(x, y + 3, z, c)),
                (there_odd, device(x, y + 1, z, 1 - c)), (there_odd, device(x, y + 3, z, 1 - c)),
                (near, device(x, y + 2, z, c)), (there, device(x, y + 2, z, 1 - c)),
            )):
                start(push(t_rows(zs, source), land, t_send.at[source, n], t_recv.at[final], target))

    gd_count = [0]

    def to_core(g, h, j):
        start(push(g_part(g, h, j), g_part(g, h, j), gd_send.at[gd_count[0]], g_sem(g, h, j), other_core))
        gd_count[0] += 1

    def cot_pair(j):
        arrived(g_part(g_own, 1 - p, j), g_sem(g_own, 1 - p, j))
        start(push(g_part(g_own, 1 - p, j), g_part(g_own, 1 - p, j), gf_send.at[j], g_sem(g_own, 1 - p, j), across))
        to_core(g_own, 1 - p, j)

    def cot_far(h, j):
        arrived(g_part(g_far, h, j), g_sem(g_far, h, j))
        to_core(g_far, h, j)

    def from_core(h):
        for g in range(2):
            for j in range(GC):
                arrived(g_part(2 * g + 1 - c, h, j), g_sem(2 * g + 1 - c, h, j))

    def split_roots(i, carry):
        part = pl.ds(pl.multiple_of(128 * i, 128), 128)
        l1[part, :], l2[part, :] = split(sbuf[part, :])
        r1[part, :], r2[part, :] = split(wbuf[part, :])
        return carry

    def multiply(t, q, h):
        ys = source_y(q)
        value = None
        for g in range(4):
            product = lax.dot_general(
                abuf[pl.ds(pl.multiple_of(TOK * (4 * ys + g) + CH * t, CH), CH), :],
                gbuf[g, h, pl.ds(pl.multiple_of(CH * t, CH), CH), :],
                (((0,), (0,)), ((), ())), preferred_element_type=F32,
            )
            value = product if value is None else value + product
        gacc[pl.ds(pl.multiple_of(FEAT * ys, FEAT), FEAT), pl.ds(pl.multiple_of(HALF * h, HALF), HALF)] += value

    def multiply_early(h):
        def body(i, carry):
            multiply(i // 4, i % 4, h)
            return carry

        return body

    along_y(0)
    cot_own(2, pair, 0)
    cot_own(2, pair, 1)
    relay_step(0)
    along_y(1)
    cot_own(2, pair, 2)
    cot_own(2, pair, 3)
    last_along_z()
    along_y(2)
    load_left.wait()
    load_right.wait()
    lax.fori_loop(0, 8, split_roots, 0)
    relay_step(1)
    last_along_y()
    sbuf[...] = jnp.zeros_like(sbuf)
    gacc[...] = jnp.zeros_like(gacc)
    gsq[...] = jnp.zeros_like(gsq)
    ssq[...] = jnp.zeros_like(ssq)
    relay_step(2)
    cot_far(p, 0)
    cot_pair(0)
    relay_step(3)
    cot_far(p, 1)
    cot_pair(1)
    relay_step(4)
    cot_far(p, 2)
    relay_step(5)
    cot_far(p, 3)
    relay_step(6)
    cot_pair(2)
    cot_far(1 - p, 0)
    relay_step(7)
    cot_pair(3)
    cot_far(1 - p, 1)
    from_core(p)
    keep_g.wait()
    lax.fori_loop(0, 4, multiply_early(p), 0)
    relay_step(8)
    cot_far(1 - p, 2)
    lax.fori_loop(4, 8, multiply_early(p), 0)
    cot_far(1 - p, 3)
    from_core(1 - p)

    def last_steps(u, carry):
        @pl.when(u < 12)
        def _():
            relay(36 + u)

        lax.fori_loop(jnp.minimum(3 * u, 8), jnp.minimum(3 * u + 3, 8), multiply_early(1 - p), 0)
        q = (u + 1) // 3 - 1
        done = jnp.logical_or(jnp.logical_or(u == 3, u == 5), jnp.logical_or(u == 8, u == 12))

        @pl.when(done)
        def _():
            ys = source_y(q)
            for g in range(4):
                @pl.when(jnp.logical_not(jnp.logical_and(q == 0, c == g % 2)))
                def _():
                    arrived(a_rows(4 * ys + g, LAST), t_recv.at[4 * ys + g])

            def body(i, inner):
                multiply(2 + i // 2, q, i % 2)
                return inner

            lax.fori_loop(0, 4, body, 0)

        at = jnp.logical_or(jnp.logical_or(u == 4, u == 6), jnp.logical_or(u == 9, u == 12))
        @pl.when(at)
        def _():
            q2 = u // 3 - 1
            ys = source_y(q2)
            columns = pl.ds(pl.multiple_of(FEAT * ys, FEAT), FEAT)
            value = gacc[columns, :]
            gsq[...] += jnp.sum(value * value, axis=0, keepdims=True)
            g1[...], g2[...] = split(value)

            def left_rows(r, inner):
                part = pl.ds(pl.multiple_of(256 * r, 256), 256)
                high = l1[part, columns]
                sbuf[part, :] += mm(high, g1[...]) + mm(high, g2[...]) + mm(l2[part, columns], g1[...])
                return inner

            lax.fori_loop(0, 4, left_rows, 0)

        return carry

    lax.fori_loop(0, 13, last_steps, 0)

    def right_rows(r, carry):
        part = pl.ds(pl.multiple_of(256 * r, 256), 256)
        high, low = split(sbuf[part, :])
        for h in range(2):
            cols = pl.ds(HALF * h, HALF)
            value = mm(high, r1[:, cols]) + mm(high, r2[:, cols]) + mm(low, r1[:, cols])
            wbuf[part, cols] = value
            ssq[:, cols] += jnp.sum(value * value, axis=0, keepdims=True)
        return carry

    lax.fori_loop(0, 4, right_rows, 0)
    count = BLK * BLK
    graft = jnp.sqrt(jnp.sum(gsq[...], axis=1, keepdims=True) / count + epsilon) / jnp.sqrt(
        jnp.sum(ssq[...], axis=1, keepdims=True) / count + epsilon
    )

    block = 4 * x_hi + 2 * c + p
    orows = BLK // OC

    def o_part(number, j):
        return out.at[pl.ds(pl.multiple_of(BLK * number + orows * j, orows), orows), :]

    def o_sem(number, j):
        return o_recv.at[number * OC + j]

    for j in range(OC + 1):
        if j < OC:
            for h in range(2):
                fin[h, pl.ds(orows * j, orows), :] = (
                    wbuf[pl.ds(orows * j, orows), pl.ds(HALF * h, HALF)] * graft
                ).astype(BF16)
        if j > 0:
            i = j - 1
            mine = fin.at[p, pl.ds(orows * i, orows), :]
            theirs = fin.at[1 - p, pl.ds(orows * i, orows), :]
            for n, (src, target) in enumerate(
                ((mine, across), (theirs, pair_across), (theirs, pair), (mine, other_core))
            ):
                start(push(src, o_part(block, i), o_send.at[n, i], o_sem(block, i), target))
            copy = pltpu.make_async_copy(mine, o_part(block, i), lo_sem.at[i])
            copy.start()
    p_core = 2 * c
    far = 4 * (1 - x_hi)
    for j in range(OC):
        for n, number in enumerate((4 * x_hi + p_core + 1 - p, far + p_core + p, far + p_core + 1 - p)):
            arrived(o_part(number, j), o_sem(number, j))
            start(push(o_part(number, j), o_part(number, j), od_send.at[n, j], o_sem(number, j), other_core))

    for j in range(OC):
        for number in (0, 1, 4, 5):
            arrived(o_part(number + 2 * (1 - c), j), o_sem(number + 2 * (1 - c), j))
        pltpu.make_async_copy(fin.at[p, pl.ds(orows * j, orows), :], o_part(block, j), lo_sem.at[j]).wait()
    for when, copy in finals:
        if when is None:
            copy.wait_send()
        else:
            pl.when(when)(copy.wait_send)

    def drain(i, carry):
        for when, copy in z_copies(i):
            pl.when(when)(copy.wait_send)
        return carry

    lax.fori_loop(0, 48, drain, 0)


def local(act, cot, left, right):
    dma = pltpu.SemaphoreType.DMA
    anywhere = pl.BlockSpec(memory_space=pl.ANY)
    return pl.pallas_call(
        kernel,
        out_shape=jax.ShapeDtypeStruct((8 * BLK, HALF), BF16),
        in_specs=[anywhere] * 4,
        out_specs=anywhere,
        scratch_shapes=[
            pltpu.VMEM((20 * TOK, FEAT), BF16),
            pltpu.VMEM((4, 2, TOK, HALF), BF16),
            pltpu.VMEM((BLK, BLK), BF16), pltpu.VMEM((BLK, BLK), BF16),
            pltpu.VMEM((BLK, BLK), BF16), pltpu.VMEM((BLK, BLK), BF16),
            pltpu.VMEM((BLK, BLK), F32), pltpu.VMEM((BLK, BLK), F32),
            pltpu.VMEM((BLK, BLK), F32),
            pltpu.VMEM((FEAT, BLK), BF16), pltpu.VMEM((FEAT, BLK), BF16),
            pltpu.VMEM((1, BLK), F32), pltpu.VMEM((1, BLK), F32),
            pltpu.VMEM((2, BLK, HALF), BF16),
            dma((2, 4)), dma((2, 4)), dma((4, 2, 3)), dma((48,)), dma((48,)), dma((48,)),
            dma((8,)), dma((3, 2)), dma((16,)), dma((2, 7)),
            dma((8 * GC,)), dma((3, GC)), dma((GC,)), dma((3 * GC,)),
            dma((8 * OC,)), dma((4, OC)), dma((3, OC)), dma((2,)), dma, dma((OC,)),
        ],
        compiler_params=pltpu.CompilerParams(
            collective_id=0, has_side_effects=True, vmem_limit_bytes=62 * 1024 * 1024
        ),
        name="shampoo",
    )(act, cot, left, right)


def solution(mesh):
    in_specs = (P("gx", "gy"), P("gx", "gy"), P(("gx", "gy"), None, None), P(("gx", "gy"), None, None))
    return jax.shard_map(local, mesh=mesh, in_specs=in_specs, out_specs=P(None, "gy"), check_vma=False)
```

time: 205 us -> 179 us (0.87)
  Pallas kernels: 198 us -> 171 us
    pallas_call x1, Pallas kernels: 198 us -> 171 us  [local(): pl.pallas_call(kernel, out_shape=jax.ShapeDtypeStruct((8 * BLK, HALF), BF...]
where the time goes in v2:
time: 179 us
  Pallas kernels  171 us (96%)
  local copies, waits for them, and re-layouts  7.32 us (4%)
    pallas_call x1, Pallas kernels, local(): pl.pallas_call(kernel, out_shape=jax.ShapeDtypeStruct((8 * BLK, HALF), BF...  171 us
    unnamed x1, local copies, waits for them, and re-layouts  7.32 us

profile of v2, /device:TPU:1, one launch (start us, length us, event | category | flops | bytes accessed | tf_op | source)
XLA Modules:
  0.0 178.6 jit_solution(8108800358007430148)
XLA Ops:
  0.0 171.3 %shampoo.1 = bf16[8192,512]{1,0:T(8,128)(2,1)} custom-call(bf16[1024,256]{1,0:T(8,128)(2,1)} %act.1, bf16[1024,512]{1,0:T(8,128)(2,1)} %cot.1, f32[1,1024,1024]{2,1,0:T(8,128)} %left.1, f32[1,1024,1024]{2,1,0:T(8,128)} %right.1), custom_call_target="tpu_custom_call" | custom-call | tf_op jit(solution)/shard_map/shampoo/pallas_call | solution.py:420
  171.3 7.3 %copy.6 = bf16[8192,512]{1,0:T(8,128)(2,1)} copy(bf16[8192,512]{1,0:T(8,128)(2,1)} %shampoo.1) | data formatting | bytes 16777216

commit v3 on v2

--- a/solution.py
+++ b/solution.py
@@ -147,6 +147,8 @@
         for s, source in enumerate(sources):
             slot = x_slot(source)
             arrived(a_rows(slot, t), x_recv.at[source, t])
+            for _, copy in z_copies(4 * t + 2 * s + c):
+                pl.when(home)(copy.start)
             final = 4 * y + 2 * source + c
             for n, (when, dy) in enumerate(((odd == 1, 1), (odd == 1, 3), (odd == 0, 2))):
                 start(
@@ -164,8 +166,13 @@
     def source_y(q):
         return (y + q + (q // 2) * (1 - 2 * (q % 2))) % 4
 
+    def step_of(step):
+        own = step < 3
+        rest = jnp.maximum(step - 3, 0)
+        return jnp.where(own, step, rest // 3), jnp.where(own, 0, 1 + rest % 3)
+
     def order(i):
-        t, q = i // 16, (i // 4) % 4
+        t, q = step_of(i // 4)
         g = 2 * ((x_hi + (i % 4) // 2) % 2) + i % 2
         return t, q, 4 * source_y(q) + g
 
@@ -185,9 +192,9 @@
         @pl.when(jnp.logical_not(held))
         def _():
             arrived(a_rows(slot, t), a_recv.at[slot * 3 + t])
-
-        for when, copy in z_copies(i):
-            pl.when(when)(copy.start)
+            for when, copy in z_copies(i):
+                pl.when(when)(copy.start)
+
         return carry
 
     def relay_step(s):
@@ -255,7 +262,7 @@
 
     def multiply_early(h):
         def body(i, carry):
-            multiply(i // 4, i % 4, h)
+            multiply(*step_of(i), h)
             return carry
 
         return body
@@ -263,44 +270,45 @@
     along_y(0)
     cot_own(2, pair, 0)
     cot_own(2, pair, 1)
-    relay_step(0)
     along_y(1)
     cot_own(2, pair, 2)
     cot_own(2, pair, 3)
+    along_y(2)
     last_along_z()
-    along_y(2)
+    relay_step(0)
+    relay_step(1)
+    last_along_y()
+    cot_far(p, 0)
+    cot_pair(0)
     load_left.wait()
     load_right.wait()
     lax.fori_loop(0, 8, split_roots, 0)
-    relay_step(1)
-    last_along_y()
+    relay_step(2)
+    cot_far(p, 1)
+    cot_pair(1)
+    cot_far(p, 2)
     sbuf[...] = jnp.zeros_like(sbuf)
     gacc[...] = jnp.zeros_like(gacc)
     gsq[...] = jnp.zeros_like(gsq)
     ssq[...] = jnp.zeros_like(ssq)
-    relay_step(2)
-    cot_far(p, 0)
-    cot_pair(0)
     relay_step(3)
-    cot_far(p, 1)
-    cot_pair(1)
+    cot_far(p, 3)
     relay_step(4)
-    cot_far(p, 2)
-    relay_step(5)
-    cot_far(p, 3)
-    relay_step(6)
     cot_pair(2)
     cot_far(1 - p, 0)
-    relay_step(7)
+    relay_step(5)
     cot_pair(3)
     cot_far(1 - p, 1)
     from_core(p)
     keep_g.wait()
+    relay_step(6)
+    cot_far(1 - p, 2)
     lax.fori_loop(0, 4, multiply_early(p), 0)
+    relay_step(7)
+    cot_far(1 - p, 3)
+    lax.fori_loop(4, 8, multiply_early(p), 0)
     relay_step(8)
-    cot_far(1 - p, 2)
-    lax.fori_loop(4, 8, multiply_early(p), 0)
-    cot_far(1 - p, 3)
+    lax.fori_loop(8, 9, multiply_early(p), 0)
     from_core(1 - p)
 
     def last_steps(u, carry):
@@ -308,7 +316,7 @@
         def _():
             relay(36 + u)
 
-        lax.fori_loop(jnp.minimum(3 * u, 8), jnp.minimum(3 * u + 3, 8), multiply_early(1 - p), 0)
+        lax.fori_loop(jnp.minimum(3 * u, 9), jnp.minimum(3 * u + 3, 9), multiply_early(1 - p), 0)
         q = (u + 1) // 3 - 1
         done = jnp.logical_or(jnp.logical_or(u == 3, u == 5), jnp.logical_or(u == 8, u == 12))
 
@@ -324,7 +332,7 @@
                 multiply(2 + i // 2, q, i % 2)
                 return inner
 
-            lax.fori_loop(0, 4, body, 0)
+            lax.fori_loop(jnp.where(q == 0, 2, 0), 4, body, 0)
 
         at = jnp.logical_or(jnp.logical_or(u == 4, u == 6), jnp.logical_or(u == 9, u == 12))
         @pl.when(at)
@@ -419,7 +427,7 @@
     anywhere = pl.BlockSpec(memory_space=pl.ANY)
     return pl.pallas_call(
         kernel,
-        out_shape=jax.ShapeDtypeStruct((8 * BLK, HALF), BF16),
+        out_shape=pltpu.VMEM((8 * BLK, HALF), BF16),
         in_specs=[anywhere] * 4,
         out_specs=anywhere,
         scratch_shapes=[
@@ -438,7 +446,7 @@
             dma((8 * OC,)), dma((4, OC)), dma((3, OC)), dma((2,)), dma, dma((OC,)),
         ],
         compiler_params=pltpu.CompilerParams(
-            collective_id=0, has_side_effects=True, vmem_limit_bytes=62 * 1024 * 1024
+            collective_id=0, has_side_effects=True, vmem_limit_bytes=46 * 1024 * 1024
         ),
         name="shampoo",
     )(act, cot, left, right)

time: 179 us -> 165 us (0.922)
  Pallas kernels: 171 us -> 161 us
  local copies, waits for them, and re-layouts: 7.32 us -> 3.4 us
    pallas_call x1, Pallas kernels: 171 us -> 161 us  [local(): pl.pallas_call(kernel, out_shape=pltpu.VMEM((8 * BLK, HALF), BF16), in_sp...]
    unnamed x1, local copies, waits for them, and re-layouts: 7.32 us -> 3.4 us
where the time goes in v3:
time: 165 us; the launch traced here: 164 us
  Pallas kernels  161 us (98%)
  local copies, waits for them, and re-layouts  3.4 us (2%)
    pallas_call x1, Pallas kernels, local(): pl.pallas_call(kernel, out_shape=pltpu.VMEM((8 * BLK, HALF), BF16), in_sp...  161 us
    unnamed x1, local copies, waits for them, and re-layouts  3.4 us

profile of v3, /device:TPU:1, one launch (start us, length us, event | category | flops | bytes accessed | tf_op | source)
XLA Modules:
  0.0 164.5 jit_solution(15531598400868936494)
XLA Ops:
  0.0 161.1 %shampoo.1 = bf16[8192,512]{1,0:T(8,128)(2,1)S(1)} custom-call(bf16[1024,256]{1,0:T(8,128)(2,1)} %act.1, bf16[1024,512]{1,0:T(8,128)(2,1)} %cot.1, f32[1,1024,1024]{2,1,0:T(8,128)} %left.1, f32[1,1024,1024]{2,1,0:T(8,128)} %right.1), custom_call_target="tpu_custom_call" | custom-call | tf_op jit(solution)/shard_map/shampoo/pallas_call | solution.py:428
  161.1 3.4 %copy.6 = bf16[8192,512]{1,0:T(8,128)(2,1)} copy(bf16[8192,512]{1,0:T(8,128)(2,1)S(1)} %shampoo.1) | data formatting | bytes 16777216

commit v4 on v3

--- a/solution.py
+++ b/solution.py
@@ -118,6 +118,7 @@
         start(push(cot.at[pl.ds(CH * j, CH), :], g_part(g_own, p, j), g_send.at[n, j], g_sem(g_own, p, j), target))
 
     for j in range(GC):
+        cot_own(2, pair, j)
         cot_own(0, across, j)
     for j in range(GC):
         cot_own(1, other_core, j)
@@ -260,6 +261,17 @@
             value = product if value is None else value + product
         gacc[pl.ds(pl.multiple_of(FEAT * ys, FEAT), FEAT), pl.ds(pl.multiple_of(HALF * h, HALF), HALF)] += value
 
+    def multiply_all(t, q):
+        ys = source_y(q)
+        values = [None, None]
+        for g in range(4):
+            turned = abuf[pl.ds(pl.multiple_of(TOK * (4 * ys + g) + CH * t, CH), CH), :].T
+            for h in range(2):
+                product = mm(turned, gbuf[g, h, pl.ds(pl.multiple_of(CH * t, CH), CH), :])
+                values[h] = product if values[h] is None else values[h] + product
+        for h in range(2):
+            gacc[pl.ds(pl.multiple_of(FEAT * ys, FEAT), FEAT), pl.ds(HALF * h, HALF)] += values[h]
+
     def multiply_early(h):
         def body(i, carry):
             multiply(*step_of(i), h)
@@ -268,16 +280,12 @@
         return body
 
     along_y(0)
-    cot_own(2, pair, 0)
-    cot_own(2, pair, 1)
     along_y(1)
-    cot_own(2, pair, 2)
-    cot_own(2, pair, 3)
     along_y(2)
     last_along_z()
+    last_along_y()
     relay_step(0)
     relay_step(1)
-    last_along_y()
     cot_far(p, 0)
     cot_pair(0)
     load_left.wait()
@@ -329,10 +337,10 @@
                     arrived(a_rows(4 * ys + g, LAST), t_recv.at[4 * ys + g])
 
             def body(i, inner):
-                multiply(2 + i // 2, q, i % 2)
+                multiply_all(2 + i, q)
                 return inner
 
-            lax.fori_loop(jnp.where(q == 0, 2, 0), 4, body, 0)
+            lax.fori_loop(jnp.where(q == 0, 1, 0), 2, body, 0)
 
         at = jnp.logical_or(jnp.logical_or(u == 4, u == 6), jnp.logical_or(u == 9, u == 12))
         @pl.when(at)

time: 165 us -> 163 us (0.988)
  Pallas kernels: 161 us -> 159 us
    pallas_call x1, Pallas kernels: 161 us -> 159 us  [local(): pl.pallas_call(kernel, out_shape=pltpu.VMEM((8 * BLK, HALF), BF16), in_sp...]
where the time goes in v4:
time: 163 us; the launch traced here: 162 us
  Pallas kernels  159 us (98%)
  local copies, waits for them, and re-layouts  3.4 us (2%)
    pallas_call x1, Pallas kernels, local(): pl.pallas_call(kernel, out_shape=pltpu.VMEM((8 * BLK, HALF), BF16), in_sp...  159 us
    unnamed x1, local copies, waits for them, and re-layouts  3.4 us

profile of v4, /device:TPU:1, one launch (start us, length us, event | category | flops | bytes accessed | tf_op | source)
XLA Modules:
  0.0 162.4 jit_solution(1841841075284274630)
XLA Ops:
  0.0 159.0 %shampoo.1 = bf16[8192,512]{1,0:T(8,128)(2,1)S(1)} custom-call(bf16[1024,256]{1,0:T(8,128)(2,1)} %act.1, bf16[1024,512]{1,0:T(8,128)(2,1)} %cot.1, f32[1,1024,1024]{2,1,0:T(8,128)} %left.1, f32[1,1024,1024]{2,1,0:T(8,128)} %right.1), custom_call_target="tpu_custom_call" | custom-call | tf_op jit(solution)/shard_map/shampoo/pallas_call | solution.py:436
  159.0 3.4 %copy.6 = bf16[8192,512]{1,0:T(8,128)(2,1)} copy(bf16[8192,512]{1,0:T(8,128)(2,1)S(1)} %shampoo.1) | data formatting | bytes 16777216
